TPU v7x, 32 devices: a whole 2x2x4 slice. The times are simulated.
32 devices in a mesh: dimer: 8 (over z, x), rep: 4 (over y, core).
Axes of the slice: x: 2, y: 2, z: 4, core: 2. Of those that a mesh axis runs over, the one named last changes fastest.
Arguments:
- integrals: bfloat16 [256, 256, 3, 128], P('dimer', 'rep'), may hold values from -0.375 to 0.375
- density: bfloat16 [256, 256], P('dimer', 'rep'), may hold values from -6 to 6
- energy_terms: bfloat16 [256, 256], P('dimer', 'rep'), may hold values from -0.0234375 to 0.0234375
- positions: float32 [3, 16384], P(None, ('dimer', 'rep')), may hold values from -0.046875 to 0.046875
- dimer_owners: int32 [256, 2], P('dimer'), may hold values from 0 to 7, all different within a row; in each aligned block of 32 rows (0 to 31, 32 to 63, ...) at most 16 rows name the same one
- dimer_local: int32 [256, 2], P('dimer'), may hold values from 0 to 31
Outputs:
- forces: float32 [3, 16384], P(None, ('dimer', 'rep'))
- energy: float32 [], replicated
- virial: float32 [], replicated
Inputs may be any that keep to these rules, and one draw needn't show every extreme that they name: `dimer_owners`: the two entries of a row differ. Among the 32 rows of one device no value stands more than 16 times, and some value stands exactly 16 times in some device's rows.
All inputs are finite; a program needn't handle non-finite values.
Results may differ from a plain program's by a relative error of at most 0.00045.
Values sent between devices are 32-bit elements; how exact they have to be, the bound alone decides.
A program may use at most 64 MiB of HBM per device.

v0:
```python
import jax
import jax.numpy as jnp
from jax import lax
from jax.sharding import PartitionSpec as P

FRAG_DEV = 32


def on_device(integrals, density, energy_terms, positions, dimer_owners, dimer_local):
    slots = integrals.shape[0]
    atoms = integrals.shape[3] // 2
    owner_count = lax.axis_size("dimer")
    highest = lax.Precision.HIGHEST
    partial_value = jnp.einsum(
        "sk,skcb->scb", density, integrals, preferred_element_type=jnp.float32
    )
    energy_part = jnp.sum(density.astype(jnp.float32) * energy_terms.astype(jnp.float32))
    energy = lax.psum(energy_part, ("dimer", "rep"))
    capacity = max(2, 4 * slots // owner_count)
    flat_owner = dimer_owners.reshape(-1)
    order = jnp.arange(2 * slots, dtype=jnp.int32)
    earlier = (flat_owner[:, None] == flat_owner[None, :]) & (order[None, :] < order[:, None])
    rank = jnp.sum(earlier.astype(jnp.int32), axis=1)
    target = flat_owner * capacity + rank
    route = (
        target[:, None] == jnp.arange(owner_count * capacity, dtype=jnp.int32)[None, :]
    ).astype(jnp.float32)
    send_blocks = jnp.einsum(
        "stn,scta->nca",
        route.reshape(slots, 2, -1),
        partial_value.reshape(slots, 3, 2, atoms),
        precision=highest,
    )
    local_hot = (
        dimer_local.reshape(-1)[:, None] == jnp.arange(FRAG_DEV, dtype=jnp.int32)[None, :]
    ).astype(jnp.float32)
    send_index = jnp.einsum("pn,pf->nf", route, local_hot, precision=highest)
    got_blocks, got_index = (
        lax.all_to_all(
            send_blocks.reshape(owner_count, capacity, 3 * atoms),
            "dimer",
            split_axis=0,
            concat_axis=0,
            tiled=True,
        ),
        lax.all_to_all(
            send_index.reshape(owner_count, capacity, FRAG_DEV),
            "dimer",
            split_axis=0,
            concat_axis=0,
            tiled=True,
        ),
    )
    lane = jnp.einsum(
        "nqf,nqca->cfa",
        got_index,
        got_blocks.reshape(owner_count, capacity, 3, atoms),
        precision=highest,
    )
    forces = lax.psum_scatter(lane, "rep", scatter_dimension=1, tiled=True).reshape(3, -1)
    virial_part = -jnp.sum(positions * forces) / 3.0
    virial = lax.psum(virial_part, ("dimer", "rep"))
    return (forces, energy, virial)


def solution(mesh):
    in_specs = (
        P("dimer", "rep", None, None),
        P("dimer", "rep"),
        P("dimer", "rep"),
        P(None, ("dimer", "rep")),
        P("dimer", None),
        P("dimer", None),
    )
    out_specs = (P(None, ("dimer", "rep")), P(), P())
    return jax.shard_map(
        on_device, mesh=mesh, in_specs=in_specs, out_specs=out_specs, check_vma=False
    )
```

profile of v0, /device:TPU:0, one launch (start us, length us, event | category | flops | bytes accessed | tf_op | source)
XLA Modules:
  0.0 101.7 jit_solution(14539411441197590968)
XLA Ops:
  7.2 0.0 copy-start
  7.2 0.9 copy.32
  8.1 0.1 eq.62
  8.2 0.2 convert_reduce_fusion
  8.4 0.8 copy.35
  9.1 0.1 eq.77
  9.2 0.3 fusion.6
  9.5 0.7 reshape.55
  10.2 7.3 %all-to-all-start.1 = ((f32[8,1,512]{2,1,0:T(1,128)}), f32[8,1,512]{2,1,0:T(1,128)S(1)}, u32[]{:S(2)}, u32[]{:S(2)}) async-start(f32[8,1,512]{2,1,0:T(1,128)} %reshape.55), calls=%async_computation.1 | async-start | bytes 32768 | tf_op jit(solution)/shard_map/all_to_all | solution.py:46
  17.5 0.1 reduce_sum.30
  17.6 0.0 copy-start.4
  17.7 1.1 %fusion.7 = f32[32,1,3,128]{3,1,2,0:T(1,128)S(1)} fusion(bf16[32,64,3,128]{3,1,2,0:T(8,128)(2,1)S(1)} %copy-done, bf16[32,64,1,1]{1,0,2,3:T(8,128)(2,1)} %bitcast.25), kind=kOutput, calls=%fused_computation.14 | convolution fusion | flops 1572864 | bytes 1626112 | tf_op jit(solution)/shard_map/sk,skcb->scb/dot_general | solution.py:14
  18.8 0.1 reshape.44
  18.9 0.1 copy.34
  19.0 0.1 reshape.50
  19.1 0.1 copy.33
  19.2 1.0 convolution_bitcast_fusion
  20.2 3.9 %all-to-all-done.1 = f32[8,1,512]{2,1,0:T(1,128)S(1)} async-done(((f32[8,1,512]{2,1,0:T(1,128)}), f32[8,1,512]{2,1,0:T(1,128)S(1)}, u32[]{:S(2)}, u32[]{:S(2)}) %all-to-all-start.1) | async-done | bytes 16416 | tf_op jit(solution)/shard_map/all_to_all | solution.py:46
  24.1 3.4 %all-to-all-start = ((f32[8,16,192]{2,1,0:T(8,128)}), f32[8,16,192]{2,1,0:T(8,128)S(1)}, u32[]{:S(2)}, u32[]{:S(2)}) async-start(f32[8,16,192]{2,1,0:T(8,128)} %convolution_bitcast_fusion), calls=%async_computation | async-start | bytes 262144 | tf_op jit(solution)/shard_map/all_to_all | solution.py:39
  27.5 0.0 reduce-scatter.2.cloned.1.call-start
  27.5 0.5 broadcast.15
  28.0 0.7 reduce
  28.7 0.1 reshape.56
  28.8 5.9 %all-to-all-done = f32[8,16,192]{2,1,0:T(8,128)S(1)} async-done(((f32[8,16,192]{2,1,0:T(8,128)}), f32[8,16,192]{2,1,0:T(8,128)S(1)}, u32[]{:S(2)}, u32[]{:S(2)}) %all-to-all-start) | async-done | bytes 98336 | tf_op jit(solution)/shard_map/all_to_all | solution.py:39
  34.7 0.1 reshape.45
  34.9 0.9 convolution_bitcast_fusion.1
  35.8 0.0 reduce-scatter.2.cloned.1.call-update
  35.8 0.6 multiply_reduce_fusion
  36.4 16.9 %reduce-scatter.2.cloned.1.call-done = f32[3,8,64]{2,1,0:T(8,128)} async-done(((f32[3,32,64]{2,1,0:T(8,128)}), f32[3,8,64]{2,1,0:T(8,128)}) %reduce-scatter.2.cloned.1.call-update) | async-done | bytes 6160 | tf_op jit(solution)/shard_map/reduce_scatter | solution.py:60
  53.3 0.8 reshape.47
  54.1 0.6 multiply_reduce_fusion.1
  55.3 39.5 %all-reduce = (f32[]{:T(128)}, f32[]{:T(128)}) all-reduce(f32[]{:T(128)} %multiply_reduce_fusion, f32[]{:T(128)S(6)} %div.3), channel_id=1, replica_groups=mesh['dimer'=8,'rep'=4] {'dimer','rep'}, use_global_device_ids=true, to_apply=%region_3.0 | all-reduce | flops 2 | bytes 16 | tf_op jit(solution)/shard_map/psum | solution.py:18
  (14 shorter events, 0.0 us)
Async XLA Ops:
  7.2 10.4 %copy-start = (bf16[32,64,3,128]{3,1,2,0:T(8,128)(2,1)S(1)}, bf16[32,64,3,128]{3,1,2,0:T(8,128)(2,1)}, u32[]{:S(2)}) copy-start(bf16[32,64,3,128]{3,1,2,0:T(8,128)(2,1)} %param.6) | copy-start | bytes 4718596
  7.2 12.0 %copy-start.5 = (s32[32,2]{0,1:T(2,128)S(1)}, s32[32,2]{0,1:T(2,128)}, u32[]{:S(2)}) copy-start(s32[32,2]{0,1:T(2,128)} %param.10) | copy-start | bytes 772
  10.2 13.9 %all-to-all-start.1 = ((f32[8,1,512]{2,1,0:T(1,128)}), f32[8,1,512]{2,1,0:T(1,128)S(1)}, u32[]{:S(2)}, u32[]{:S(2)}) async-start(f32[8,1,512]{2,1,0:T(1,128)} %reshape.55), calls=%async_computation.1 | async-start | bytes 32768 | tf_op jit(solution)/shard_map/all_to_all | solution.py:46
  17.6 18.2 %copy-start.1 = (bf16[32,64]{1,0:T(8,128)(2,1)S(1)}, bf16[32,64]{1,0:T(8,128)(2,1)}, u32[]{:S(2)}) copy-start(bf16[32,64]{1,0:T(8,128)(2,1)} %param.7) | copy-start | bytes 12292
  17.6 18.2 %copy-start.3 = (bf16[32,64]{1,0:T(8,128)(2,1)S(1)}, bf16[32,64]{1,0:T(8,128)(2,1)}, u32[]{:S(2)}) copy-start(bf16[32,64]{1,0:T(8,128)(2,1)} %param.8) | copy-start | bytes 12292
  17.6 36.4 %copy-start.4 = (f32[3,512]{1,0:T(4,128)S(1)}, f32[3,512]{1,0:T(4,128)}, u32[]{:S(2)}) copy-start(f32[3,512]{1,0:T(4,128)} %param.9) | copy-start | bytes 18436
  24.1 10.7 %all-to-all-start = ((f32[8,16,192]{2,1,0:T(8,128)}), f32[8,16,192]{2,1,0:T(8,128)S(1)}, u32[]{:S(2)}, u32[]{:S(2)}) async-start(f32[8,16,192]{2,1,0:T(8,128)} %convolution_bitcast_fusion), calls=%async_computation | async-start | bytes 262144 | tf_op jit(solution)/shard_map/all_to_all | solution.py:39
  27.5 25.8 %reduce-scatter.2.cloned.1.call-start = ((), (), s32[]{:S(2)}) async-start(), calls=%async_computation.3 | async-start | bytes 61440 | tf_op jit(solution)/shard_map/reduce_scatter | solution.py:60
  54.1 40.8 %copy-start.2 = (f32[3,512]{1,0:T(4,128)}, f32[3,512]{1,0:T(4,128)S(1)}, u32[]{:S(2)}) copy-start(f32[3,512]{1,0:T(4,128)S(1)} %reshape.47) | copy-start | bytes 18436
Sparse Core Ops, SparseCore 0:
  35.9 17.3 reduce-scatter.1
where the time goes:
time: 102 us
  blocking collectives  39.5 us (39%)
  waiting for transfers between devices  26.7 us (26%)
  between operations  14.8 us (15%)
  starting transfers between devices  10.7 us (10%)
  local copies, waits for them, and re-layouts  4.59 us (4%)
  matrix products  3.26 us (3%)
  other arithmetic  2.08 us (2%)
    psum x1, blocking collectives, on_device(): energy = lax.psum(energy_part, ('dimer', 'rep'))  39.5 us
    reduce_scatter x1, waiting for transfers between devices, on_device(): lax.psum_scatter(lane, 'rep', scatter_dimension=1, tiled=True)  16.9 us
    all_to_all x1, starting transfers between devices, on_device(): lax.all_to_all(send_index.reshape(owner_count, capacity, FRAG_DEV), 'dime...  7.28 us
    all_to_all x1, waiting for transfers between devices, on_device(): lax.all_to_all(send_blocks.reshape(owner_count, capacity, 3 * atoms), 'di...  5.95 us
    all_to_all x1, waiting for transfers between devices, on_device(): lax.all_to_all(send_index.reshape(owner_count, capacity, FRAG_DEV), 'dime...  3.91 us
    all_to_all x1, starting transfers between devices, on_device(): lax.all_to_all(send_blocks.reshape(owner_count, capacity, 3 * atoms), 'di...  3.37 us
    unnamed x16, local copies, waits for them, and re-layouts  2.46 us
  transfers between devices with their start and end apart: 3, of which 3 were waited for; matrix products, arithmetic and copies ran while one was open for 4% of the time, Pallas kernels for 0%

commit v1 on v0

v1 whole, which is shorter than its diff:
```python
import functools

import jax
import jax.numpy as jnp
from jax import lax
from jax.experimental import pallas as pl
from jax.experimental.pallas import tpu as pltpu
from jax.sharding import PartitionSpec as P

MESH = pl.DeviceIdType.MESH
F32, BF16 = jnp.float32, jnp.bfloat16


def kernel(
    n_d, n_r, integ, dens, eterm, pos, owner, local, forces, scalars,
    ibuf, dbuf, in_a, acc, in_b, posb, in_p, sbuf, in_s,
    isem, a_send, a_recv, b_send, b_recv, p_send, p_recv, s_send, s_recv,
):
    slots, terms = dens.shape
    lanes = ibuf.shape[3]
    half = lanes // 2
    pairs = pos.shape[1] // lanes
    per_rep = 2 * pairs
    n_all = n_d * n_r
    rows = n_r * n_d * pairs
    d, r = lax.axis_index("dimer"), lax.axis_index("rep")
    me = d * n_r + r

    def device(step):
        peer = lax.rem(me + step, n_all)
        return (peer // n_r, lax.rem(peer, n_r))

    loads = [pltpu.make_async_copy(integ.at[:, c], ibuf.at[c], isem.at[c]) for c in range(3)]
    for load in loads:
        load.start()

    barrier = pltpu.get_barrier_semaphore()

    def greet(step, carry):
        pl.semaphore_signal(barrier, inc=1, device_id=device(step), device_id_type=MESH)
        return carry

    lax.fori_loop(1, n_all, greet, 0)

    weights = dens[...].astype(F32)
    span = slots * terms
    lane = lax.broadcasted_iota(jnp.int32, (slots, span), 1)
    first = lax.broadcasted_iota(jnp.int32, (slots, span), 0) * terms
    spread = jnp.concatenate([weights] * slots, axis=1)
    diagonal = jnp.where((lane >= first) & (lane < first + terms), spread, 0.0).astype(BF16)

    name, index = owner[...], local[...]
    rep = jnp.zeros_like(index)
    for bound in range(1, n_r):
        rep = rep + (index >= bound * per_rep).astype(jnp.int32)
    rest = index - rep * per_rep
    target = rep * (n_d * pairs) + name * pairs + lax.shift_right_logical(rest, 1)
    parity = rest & 1
    keys = []
    for t in range(2):
        for h in range(2):
            keys.append(jnp.where(parity[t : t + 1] == h, target[t : t + 1], -1))
    key = jnp.concatenate(keys, axis=1)
    place = lax.broadcasted_iota(jnp.int32, (rows, 4 * slots), 0)
    hot = jnp.where(place == key, 1.0, 0.0).astype(BF16)
    hot = jnp.concatenate([hot] * 3, axis=1)

    for c in range(3):
        for j in range(pairs):
            posb[c * pairs + j : c * pairs + j + 1] = pos[c : c + 1, j * lanes : (j + 1) * lanes]
    energy = jnp.sum(weights * eterm[...].astype(F32), axis=0, keepdims=True)
    sbuf[1:2] = jnp.concatenate([energy, jnp.zeros((1, lanes - terms), F32)], axis=1)

    side = lax.broadcasted_iota(jnp.int32, (slots, lanes), 1) >= half
    for c in range(3):
        loads[c].wait()
        grad = jnp.dot(
            diagonal, ibuf[c].reshape(span, lanes), preferred_element_type=F32
        )
        swap = pltpu.roll(grad, half, 1)
        spreads = jnp.concatenate(
            [
                jnp.where(side, 0.0, grad),
                jnp.where(side, swap, 0.0),
                jnp.where(side, 0.0, swap),
                jnp.where(side, grad, 0.0),
            ],
            axis=0,
        )
        high = spreads.astype(BF16)
        left = spreads - high.astype(F32)
        middle = left.astype(BF16)
        low = (left - middle.astype(F32)).astype(BF16)
        placed = jnp.dot(
            hot, jnp.concatenate([high, middle, low], axis=0), preferred_element_type=F32
        )
        for q in range(n_r):
            dbuf[q, c] = placed[q * n_d * pairs : (q + 1) * n_d * pairs]

    pl.semaphore_wait(barrier, n_all - 1)

    a_copies = []
    for k in range(1, n_r):
        to = lax.rem(r + k, n_r)
        a_copies.append(
            pltpu.make_async_remote_copy(
                src_ref=dbuf.at[to], dst_ref=in_a.at[k - 1],
                send_sem=a_send.at[k - 1], recv_sem=a_recv.at[k - 1],
                device_id=(d, to), device_id_type=MESH,
            )
        )
    for copy in a_copies:
        copy.start()

    def p_copy(k):
        return pltpu.make_async_remote_copy(
            src_ref=posb, dst_ref=in_p.at[k - 1],
            send_sem=p_send.at[k - 1], recv_sem=p_recv.at[k - 1],
            device_id=(lax.rem(d + k, n_d), r), device_id_type=MESH,
        )

    def b_copy(k):
        to = lax.rem(d + k, n_d)
        return pltpu.make_async_remote_copy(
            src_ref=acc.at[to], dst_ref=in_b.at[k - 1],
            send_sem=b_send.at[k - 1], recv_sem=b_recv.at[k - 1],
            device_id=(to, r), device_id_type=MESH,
        )

    def s_copy(k):
        return pltpu.make_async_remote_copy(
            src_ref=sbuf, dst_ref=in_s.at[k - 1],
            send_sem=s_send.at[k - 1], recv_sem=s_recv.at[k - 1],
            device_id=device(k), device_id_type=MESH,
        )

    def each(last, act):
        def body(k, carry):
            act(k)
            return carry

        lax.fori_loop(1, last, body, 0)

    each(n_d, lambda k: p_copy(k).start())
    for copy in a_copies:
        copy.wait_recv()
    for c in range(3):
        total = dbuf[r, c]
        for k in range(n_r - 1):
            total = total + in_a[k, c]
        for o in range(n_d):
            acc[o, c * pairs : (c + 1) * pairs] = total[o * pairs : (o + 1) * pairs]
    each(n_d, lambda k: b_copy(k).start())
    each(n_d, lambda k: p_copy(k).wait_recv())

    def virial_of(k, carry):
        return carry + acc[lax.rem(d - k + n_d, n_d)] * in_p[k - 1]

    products = lax.fori_loop(1, n_d, virial_of, acc[d] * posb[...])
    sbuf[0:1] = jnp.sum(products, axis=0, keepdims=True)
    each(n_all, lambda k: s_copy(k).start())

    each(n_d, lambda k: b_copy(k).wait_recv())
    total = lax.fori_loop(1, n_d, lambda k, carry: carry + in_b[k - 1], acc[d])
    for c in range(3):
        for j in range(pairs):
            forces[c : c + 1, j * lanes : (j + 1) * lanes] = total[c * pairs + j : c * pairs + j + 1]

    each(n_all, lambda k: s_copy(k).wait_recv())
    both = lax.fori_loop(1, n_all, lambda k, carry: carry + in_s[k - 1], sbuf[...])
    both = jnp.sum(both, axis=1, keepdims=True)
    row = lax.broadcasted_iota(jnp.int32, both.shape, 0)
    both = jnp.where(row == 0, both / -3.0, both)
    scalars[...] = jnp.broadcast_to(both, scalars.shape)

    for copy in a_copies:
        copy.wait_send()
    each(n_d, lambda k: p_copy(k).wait_send())
    each(n_d, lambda k: b_copy(k).wait_send())
    each(n_all, lambda k: s_copy(k).wait_send())


def on_device(n_d, n_r, integrals, density, energy_terms, positions, owners, local):
    slots, terms, _, lanes = integrals.shape
    pairs = positions.shape[1] // lanes
    n_all = n_d * n_r
    vmem = pl.BlockSpec(memory_space=pltpu.VMEM)
    dma = pltpu.SemaphoreType.DMA
    forces, scalars = pl.pallas_call(
        functools.partial(kernel, n_d, n_r),
        out_shape=(
            jax.ShapeDtypeStruct(positions.shape, F32),
            jax.ShapeDtypeStruct((2, lanes), F32),
        ),
        in_specs=[pl.BlockSpec(memory_space=pl.ANY)] + [vmem] * 5,
        out_specs=(vmem, vmem),
        scratch_shapes=[
            pltpu.VMEM((3, slots, terms, lanes), BF16),
            pltpu.VMEM((n_r, 3, n_d * pairs, lanes), F32),
            pltpu.VMEM((n_r - 1, 3, n_d * pairs, lanes), F32),
            pltpu.VMEM((n_d, 3 * pairs, lanes), F32),
            pltpu.VMEM((n_d - 1, 3 * pairs, lanes), F32),
            pltpu.VMEM((3 * pairs, lanes), F32),
            pltpu.VMEM((n_d - 1, 3 * pairs, lanes), F32),
            pltpu.VMEM((2, lanes), F32),
            pltpu.VMEM((n_all - 1, 2, lanes), F32),
            dma((3,)),
            dma((n_r - 1,)), dma((n_r - 1,)),
            dma((n_d - 1,)), dma((n_d - 1,)),
            dma((n_d - 1,)), dma((n_d - 1,)),
            dma((n_all - 1,)), dma((n_all - 1,)),
        ],
        compiler_params=pltpu.CompilerParams(collective_id=0, has_side_effects=True),
    )(
        jnp.transpose(integrals, (0, 2, 1, 3)), density, energy_terms, positions,
        owners.T, local.T,
    )
    return forces, scalars[1, 0], scalars[0, 0]


def solution(mesh):
    in_specs = (
        P("dimer", "rep", None, None),
        P("dimer", "rep"),
        P("dimer", "rep"),
        P(None, ("dimer", "rep")),
        P("dimer", None),
        P("dimer", None),
    )
    out_specs = (P(None, ("dimer", "rep")), P(), P())
    return jax.shard_map(
        functools.partial(on_device, mesh.shape["dimer"], mesh.shape["rep"]),
        mesh=mesh, in_specs=in_specs, out_specs=out_specs, check_vma=False,
    )
```

time: 102 us -> 21.7 us (0.21)
  blocking collectives: 39.5 us -> 0 us
  waiting for transfers between devices: 26.7 us -> 0 us
  Pallas kernels: 0 us -> 18.2 us
  between operations: 14.8 us -> 0.64 us
  starting transfers between devices: 10.7 us -> 0 us
  matrix products: 3.26 us -> 0 us
  other arithmetic: 2.08 us -> 0 us
  local copies, waits for them, and re-layouts: 4.59 us -> 2.56 us
    psum x1 -> x0, blocking collectives: 39.5 us -> none  [on_device(): energy = lax.psum(energy_part, ('dimer', 'rep'))]
    pallas_call x0 -> x1, Pallas kernels: none -> 18.2 us  [on_device(): pl.pallas_call(functools.partial(kernel, n_d, n_r), out_shape=(jax.ShapeD...]
    reduce_scatter x1 -> x0, waiting for transfers between devices: 16.9 us -> none  [on_device(): lax.psum_scatter(lane, 'rep', scatter_dimension=1, tiled=True)]
    all_to_all x2 -> x0, starting transfers between devices: 10.7 us -> none  [the longest x1 7.28 us: on_device(): lax.all_to_all(send_index.reshape(owner_count, capacity, FRAG_DEV), 'dime...]
    all_to_all x2 -> x0, waiting for transfers between devices: 9.85 us -> none  [the longest x1 5.95 us: on_device(): lax.all_to_all(send_blocks.reshape(owner_count, capacity, 3 * atoms), 'di...]
    dot_general x4 -> x0, matrix products: 3.26 us -> none  [the longest x1 1.11 us: on_device(): jnp.einsum('sk,skcb->scb', density, integrals, preferred_element_type=jnp...]
    reduce_sum x3 -> x0, other arithmetic: 1.39 us -> none  [the longest x1 0.61 us: on_device(): jnp.sum(density.astype(jnp.float32) * energy_terms.astype(jnp.float32))]
    slice x0 -> x1, local copies, waits for them, and re-layouts: none -> 1.26 us  [on_device(): return (forces, scalars[1, 0], scalars[0, 0])]
  transfers between devices with their start and end apart: 3 -> 0, of which waited for: 3 -> 0; matrix products, arithmetic and copies ran while one was open for 4% -> 0% of each run, Pallas kernels for 0% -> 0%
where the time goes in v1:
time: 21.7 us; the launch traced here: 21.4 us
  Pallas kernels  18.2 us (84%)
  local copies, waits for them, and re-layouts  2.56 us (12%)
  between operations  0.64 us (3%)
    pallas_call x1, Pallas kernels, on_device(): pl.pallas_call(functools.partial(kernel, n_d, n_r), out_shape=(jax.ShapeD...  18.2 us
    unnamed x1, local copies, waits for them, and re-layouts  1.3 us
    slice x1, local copies, waits for them, and re-layouts, on_device(): return (forces, scalars[1, 0], scalars[0, 0])  1.26 us

profile of v1, /device:TPU:0, one launch (start us, length us, event | category | flops | bytes accessed | tf_op | source)
XLA Modules:
  0.0 21.4 jit_solution(6702827643430083369)
XLA Ops:
  0.6 18.2 %shard_map.85 = (f32[3,512]{1,0:T(4,128)}, f32[2,128]{1,0:T(2,128)}) custom-call(bf16[32,3,64,128]{3,2,1,0:T(8,128)(2,1)} %bitcast.5, bf16[32,64]{1,0:T(8,128)(2,1)} %dens.1, bf16[32,64]{1,0:T(8,128)(2,1)} %eterm.1, f32[3,512]{1,0:T(4,128)} %pos.1, s32[2,32]{1,0:T(2,128)} %bitcast.6, s32[2,32]{1,0:T(2,128)} %bitcast.7), custom_call_target="tpu_custom_call" | custom-call | tf_op jit(solution)/shard_map/pallas_call | solution.py:189
  18.8 1.3 %fusion = (f32[1,1]{1,0:T(1,128)}, f32[1,1]{1,0:T(1,128)}) fusion(f32[2,128]{1,0:T(2,128)} %get-tuple-element.6), kind=kLoop, calls=%fused_computation | loop fusion | bytes 16 | tf_op jit(solution)/shard_map/slice | solution.py:218
  20.1 1.3 %copy.10 = f32[3,512]{1,0:T(4,128)} copy(f32[3,512]{1,0:T(4,128)} %get-tuple-element.12) | data formatting | bytes 12288

commit v2 on v1

--- a/solution.py
+++ b/solution.py
@@ -12,10 +12,13 @@
 
 
 def kernel(
-    n_d, n_r, integ, dens, eterm, pos, owner, local, forces, scalars,
-    ibuf, dbuf, in_a, acc, in_b, posb, in_p, sbuf, in_s,
-    isem, a_send, a_recv, b_send, b_recv, p_send, p_recv, s_send, s_recv,
+    n_d, n_r, integ, *refs,
 ):
+    smalls, (forces, scalars), (dens, eterm, pos, owner, local) = refs[:5], refs[5:7], refs[7:12]
+    (
+        ibuf, dbuf, in_a, acc, in_b, posb, in_p, sbuf, in_s,
+        isem, a_send, a_recv, b_send, b_recv, p_send, p_recv, s_send, s_recv,
+    ) = refs[12:]
     slots, terms = dens.shape
     lanes = ibuf.shape[3]
     half = lanes // 2
@@ -31,8 +34,12 @@
         return (peer // n_r, lax.rem(peer, n_r))
 
     loads = [pltpu.make_async_copy(integ.at[:, c], ibuf.at[c], isem.at[c]) for c in range(3)]
-    for load in loads:
-        load.start()
+    fetches = [
+        pltpu.make_async_copy(source, held, isem.at[3 + i])
+        for i, (source, held) in enumerate(zip(smalls, (dens, eterm, pos, owner, local)))
+    ]
+    for copy in loads + fetches:
+        copy.start()
 
     barrier = pltpu.get_barrier_semaphore()
 
@@ -41,6 +48,9 @@
         return carry
 
     lax.fori_loop(1, n_all, greet, 0)
+
+    for fetch in fetches:
+        fetch.wait()
 
     weights = dens[...].astype(F32)
     span = slots * terms
@@ -184,17 +194,27 @@
     slots, terms, _, lanes = integrals.shape
     pairs = positions.shape[1] // lanes
     n_all = n_d * n_r
+    room = 2 * (2 * integrals.size + 4 * lanes * 8 * n_d * n_r * (3 * pairs + 4)) + 2**21
     vmem = pl.BlockSpec(memory_space=pltpu.VMEM)
     dma = pltpu.SemaphoreType.DMA
+    inputs = (
+        jnp.transpose(integrals, (0, 2, 1, 3)), density, energy_terms, positions,
+        owners.T, local.T,
+    )
     forces, scalars = pl.pallas_call(
         functools.partial(kernel, n_d, n_r),
         out_shape=(
             jax.ShapeDtypeStruct(positions.shape, F32),
             jax.ShapeDtypeStruct((2, lanes), F32),
         ),
-        in_specs=[pl.BlockSpec(memory_space=pl.ANY)] + [vmem] * 5,
+        in_specs=[pl.BlockSpec(memory_space=pltpu.HBM)] * 6,
         out_specs=(vmem, vmem),
         scratch_shapes=[
+            pltpu.VMEM(density.shape, BF16),
+            pltpu.VMEM(energy_terms.shape, BF16),
+            pltpu.VMEM(positions.shape, F32),
+            pltpu.VMEM((2, slots), jnp.int32),
+            pltpu.VMEM((2, slots), jnp.int32),
             pltpu.VMEM((3, slots, terms, lanes), BF16),
             pltpu.VMEM((n_r, 3, n_d * pairs, lanes), F32),
             pltpu.VMEM((n_r - 1, 3, n_d * pairs, lanes), F32),
@@ -204,17 +224,16 @@
             pltpu.VMEM((n_d - 1, 3 * pairs, lanes), F32),
             pltpu.VMEM((2, lanes), F32),
             pltpu.VMEM((n_all - 1, 2, lanes), F32),
-            dma((3,)),
+            dma((8,)),
             dma((n_r - 1,)), dma((n_r - 1,)),
             dma((n_d - 1,)), dma((n_d - 1,)),
             dma((n_d - 1,)), dma((n_d - 1,)),
             dma((n_all - 1,)), dma((n_all - 1,)),
         ],
-        compiler_params=pltpu.CompilerParams(collective_id=0, has_side_effects=True),
-    )(
-        jnp.transpose(integrals, (0, 2, 1, 3)), density, energy_terms, positions,
-        owners.T, local.T,
-    )
+        compiler_params=pltpu.CompilerParams(
+            collective_id=0, has_side_effects=True, vmem_limit_bytes=room
+        ),
+    )(*[pltpu.with_memory_space_constraint(x, pltpu.HBM) for x in inputs])
     return forces, scalars[1, 0], scalars[0, 0]
 
 

time: 21.7 us -> 18.9 us (0.87)
  local copies, waits for them, and re-layouts: 2.56 us -> 1.12 us
  Pallas kernels: 18.2 us -> 17 us
    pallas_call x1, Pallas kernels: 18.2 us -> 17 us  [on_device(): pl.pallas_call(functools.partial(kernel, n_d, n_r), out_shape=(jax.ShapeD...]
    slice x1, local copies, waits for them, and re-layouts: 1.26 us -> 0.52 us  [on_device(): return (forces, scalars[1, 0], scalars[0, 0])]
    unnamed x1, local copies, waits for them, and re-layouts: 1.3 us -> 0.6 us
where the time goes in v2:
time: 18.9 us; the launch traced here: 18.7 us
  Pallas kernels  17 us (90%)
  local copies, waits for them, and re-layouts  1.12 us (6%)
  between operations  0.64 us (3%)
    pallas_call x1, Pallas kernels, on_device(): pl.pallas_call(functools.partial(kernel, n_d, n_r), out_shape=(jax.ShapeD...  17 us
    unnamed x1, local copies, waits for them, and re-layouts  0.6 us
    slice x1, local copies, waits for them, and re-layouts, on_device(): return (forces, scalars[1, 0], scalars[0, 0])  0.52 us

profile of v2, /device:TPU:0, one launch (start us, length us, event | category | flops | bytes accessed | tf_op | source)
XLA Modules:
  0.0 18.7 jit_solution(17451566178565310875)
XLA Ops:
  0.6 17.0 %shard_map.85 = (f32[3,512]{1,0:T(4,128)S(1)}, f32[2,128]{1,0:T(2,128)S(1)}) custom-call(bf16[32,3,64,128]{3,2,1,0:T(8,128)(2,1)} %bitcast.5, bf16[32,64]{1,0:T(8,128)(2,1)} %refs_0_.1, bf16[32,64]{1,0:T(8,128)(2,1)} %refs_1_.1, f32[3,512]{1,0:T(4,128)} %refs_2_.1, s32[2,32]{1,0:T(2,128)} %bitcast.6, s32[2,32]{1,0:T(2,128)} %bitcast.7), custom_call_target="tpu_custom_call" | custom-call | tf_op jit(solution)/shard_map/pallas_call | solution.py:204
  17.6 0.5 %fusion = (f32[1,1]{1,0:T(1,128)}, f32[1,1]{1,0:T(1,128)}) fusion(f32[2,128]{1,0:T(2,128)S(1)} %get-tuple-element.6), kind=kLoop, calls=%fused_computation | loop fusion | bytes 16 | tf_op jit(solution)/shard_map/slice | solution.py:237
  18.1 0.6 %copy.10 = f32[3,512]{1,0:T(4,128)} copy(f32[3,512]{1,0:T(4,128)S(1)} %get-tuple-element.12) | data formatting | bytes 12288

commit v3 on v2

--- a/solution.py
+++ b/solution.py
@@ -29,9 +29,18 @@
     d, r = lax.axis_index("dimer"), lax.axis_index("rep")
     me = d * n_r + r
 
-    def device(step):
-        peer = lax.rem(me + step, n_all)
-        return (peer // n_r, lax.rem(peer, n_r))
+    def partner(step, mine, count):
+        flip = (2 * mine) // count
+        at = flip * step + (1 - flip) * (count - 2 - step)
+        peer = at + (at + count - mine) // count
+        return peer, mine - (mine + count - 1 - peer) // count
+
+    def each(count, act):
+        if count <= 64:
+            for k in range(count - 1):
+                act(k)
+        else:
+            lax.fori_loop(0, count - 1, lambda k, carry: (act(k), carry)[1], 0)
 
     loads = [pltpu.make_async_copy(integ.at[:, c], ibuf.at[c], isem.at[c]) for c in range(3)]
     fetches = [
@@ -43,11 +52,13 @@
 
     barrier = pltpu.get_barrier_semaphore()
 
-    def greet(step, carry):
-        pl.semaphore_signal(barrier, inc=1, device_id=device(step), device_id_type=MESH)
-        return carry
-
-    lax.fori_loop(1, n_all, greet, 0)
+    def greet(k):
+        peer, _ = partner(k, me, n_all)
+        pl.semaphore_signal(
+            barrier, inc=1, device_id=(peer // n_r, lax.rem(peer, n_r)), device_id_type=MESH
+        )
+
+    each(n_all, greet)
 
     for fetch in fetches:
         fetch.wait()
@@ -122,34 +133,30 @@
     for copy in a_copies:
         copy.start()
 
+    def over_dimer(k, source, held, send, recv):
+        peer, slot = partner(k, d, n_d)
+        return pltpu.make_async_remote_copy(
+            src_ref=source(peer), dst_ref=held.at[slot],
+            send_sem=send.at[k], recv_sem=recv.at[slot],
+            device_id=(peer, r), device_id_type=MESH,
+        )
+
+    def arrived(k, held, recv):
+        pltpu.make_async_copy(held.at[k], held.at[k], recv.at[k]).wait()
+
     def p_copy(k):
+        return over_dimer(k, lambda peer: posb, in_p, p_send, p_recv)
+
+    def b_copy(k):
+        return over_dimer(k, lambda peer: acc.at[peer], in_b, b_send, b_recv)
+
+    def s_copy(k):
+        peer, slot = partner(k, me, n_all)
         return pltpu.make_async_remote_copy(
-            src_ref=posb, dst_ref=in_p.at[k - 1],
-            send_sem=p_send.at[k - 1], recv_sem=p_recv.at[k - 1],
-            device_id=(lax.rem(d + k, n_d), r), device_id_type=MESH,
-        )
-
-    def b_copy(k):
-        to = lax.rem(d + k, n_d)
-        return pltpu.make_async_remote_copy(
-            src_ref=acc.at[to], dst_ref=in_b.at[k - 1],
-            send_sem=b_send.at[k - 1], recv_sem=b_recv.at[k - 1],
-            device_id=(to, r), device_id_type=MESH,
-        )
-
-    def s_copy(k):
-        return pltpu.make_async_remote_copy(
-            src_ref=sbuf, dst_ref=in_s.at[k - 1],
-            send_sem=s_send.at[k - 1], recv_sem=s_recv.at[k - 1],
-            device_id=device(k), device_id_type=MESH,
-        )
-
-    def each(last, act):
-        def body(k, carry):
-            act(k)
-            return carry
-
-        lax.fori_loop(1, last, body, 0)
+            src_ref=sbuf, dst_ref=in_s.at[slot],
+            send_sem=s_send.at[k], recv_sem=s_recv.at[slot],
+            device_id=(peer // n_r, lax.rem(peer, n_r)), device_id_type=MESH,
+        )
 
     each(n_d, lambda k: p_copy(k).start())
     for copy in a_copies:
@@ -161,33 +168,37 @@
         for o in range(n_d):
             acc[o, c * pairs : (c + 1) * pairs] = total[o * pairs : (o + 1) * pairs]
     each(n_d, lambda k: b_copy(k).start())
-    each(n_d, lambda k: p_copy(k).wait_recv())
+    each(n_d, lambda k: arrived(k, in_p, p_recv))
 
     def virial_of(k, carry):
-        return carry + acc[lax.rem(d - k + n_d, n_d)] * in_p[k - 1]
-
-    products = lax.fori_loop(1, n_d, virial_of, acc[d] * posb[...])
+        return carry + acc[k + (k + n_d - d) // n_d] * in_p[k]
+
+    products = acc[d] * posb[...]
+    if n_d <= 64:
+        for k in range(n_d - 1):
+            products = virial_of(k, products)
+    else:
+        products = lax.fori_loop(0, n_d - 1, virial_of, products)
     sbuf[0:1] = jnp.sum(products, axis=0, keepdims=True)
     each(n_all, lambda k: s_copy(k).start())
-
-    each(n_d, lambda k: b_copy(k).wait_recv())
-    total = lax.fori_loop(1, n_d, lambda k, carry: carry + in_b[k - 1], acc[d])
-    for c in range(3):
-        for j in range(pairs):
-            forces[c : c + 1, j * lanes : (j + 1) * lanes] = total[c * pairs + j : c * pairs + j + 1]
-
-    each(n_all, lambda k: s_copy(k).wait_recv())
-    both = lax.fori_loop(1, n_all, lambda k, carry: carry + in_s[k - 1], sbuf[...])
-    both = jnp.sum(both, axis=1, keepdims=True)
-    row = lax.broadcasted_iota(jnp.int32, both.shape, 0)
-    both = jnp.where(row == 0, both / -3.0, both)
-    scalars[...] = jnp.broadcast_to(both, scalars.shape)
 
     for copy in a_copies:
         copy.wait_send()
     each(n_d, lambda k: p_copy(k).wait_send())
+    each(n_d, lambda k: arrived(k, in_b, b_recv))
+    total = acc[d] + jnp.sum(in_b[...], axis=0)
+    for c in range(3):
+        for j in range(pairs):
+            forces[c : c + 1, j * lanes : (j + 1) * lanes] = total[c * pairs + j : c * pairs + j + 1]
     each(n_d, lambda k: b_copy(k).wait_send())
     each(n_all, lambda k: s_copy(k).wait_send())
+
+    each(n_all, lambda k: arrived(k, in_s, s_recv))
+    both = sbuf[...] + jnp.sum(in_s[...], axis=0)
+    both = jnp.sum(both, axis=1, keepdims=True)
+    row = lax.broadcasted_iota(jnp.int32, both.shape, 0)
+    both = jnp.where(row == 0, both * (-1.0 / 3.0), both)
+    scalars[...] = jnp.broadcast_to(both, scalars.shape)
 
 
 def on_device(n_d, n_r, integrals, density, energy_terms, positions, owners, local):

time: 18.9 us -> 17.9 us (0.947)
  Pallas kernels: 17 us -> 16 us
    pallas_call x1, Pallas kernels: 17 us -> 16 us  [on_device(): pl.pallas_call(functools.partial(kernel, n_d, n_r), out_shape=(jax.ShapeD...]
where the time goes in v3:
time: 17.9 us; the launch traced here: 17.8 us
  Pallas kernels  16 us (89%)
  local copies, waits for them, and re-layouts  1.12 us (6%)
  between operations  0.64 us (4%)
    pallas_call x1, Pallas kernels, on_device(): pl.pallas_call(functools.partial(kernel, n_d, n_r), out_shape=(jax.ShapeD...  16 us
    unnamed x1, local copies, waits for them, and re-layouts  0.6 us
    slice x1, local copies, waits for them, and re-layouts, on_device(): return (forces, scalars[1, 0], scalars[0, 0])  0.52 us

profile of v3, /device:TPU:0, one launch (start us, length us, event | category | flops | bytes accessed | tf_op | source)
XLA Modules:
  0.0 17.8 jit_solution(10637806400769914654)
XLA Ops:
  0.6 16.0 %shard_map.85 = (f32[3,512]{1,0:T(4,128)S(1)}, f32[2,128]{1,0:T(2,128)S(1)}) custom-call(bf16[32,3,64,128]{3,2,1,0:T(8,128)(2,1)} %bitcast.5, bf16[32,64]{1,0:T(8,128)(2,1)} %refs_0_.1, bf16[32,64]{1,0:T(8,128)(2,1)} %refs_1_.1, f32[3,512]{1,0:T(4,128)} %refs_2_.1, s32[2,32]{1,0:T(2,128)} %bitcast.6, s32[2,32]{1,0:T(2,128)} %bitcast.7), custom_call_target="tpu_custom_call" | custom-call | tf_op jit(solution)/shard_map/pallas_call | solution.py:215
  16.7 0.5 %fusion = (f32[1,1]{1,0:T(1,128)}, f32[1,1]{1,0:T(1,128)}) fusion(f32[2,128]{1,0:T(2,128)S(1)} %get-tuple-element.6), kind=kLoop, calls=%fused_computation | loop fusion | bytes 16 | tf_op jit(solution)/shard_map/slice | solution.py:248
  17.2 0.6 %copy.10 = f32[3,512]{1,0:T(4,128)} copy(f32[3,512]{1,0:T(4,128)S(1)} %get-tuple-element.12) | data formatting | bytes 12288

commit v4 on v3

--- a/solution.py
+++ b/solution.py
@@ -52,13 +52,11 @@
 
     barrier = pltpu.get_barrier_semaphore()
 
-    def greet(k):
-        peer, _ = partner(k, me, n_all)
-        pl.semaphore_signal(
-            barrier, inc=1, device_id=(peer // n_r, lax.rem(peer, n_r)), device_id_type=MESH
-        )
-
-    each(n_all, greet)
+    def greet(*device):
+        pl.semaphore_signal(barrier, inc=1, device_id=device, device_id_type=MESH)
+
+    each(n_d, lambda k: greet(partner(k, d, n_d)[0], r))
+    each(n_r, lambda k: greet(d, partner(k, r, n_r)[0]))
 
     for fetch in fetches:
         fetch.wait()
@@ -118,7 +116,7 @@
         for q in range(n_r):
             dbuf[q, c] = placed[q * n_d * pairs : (q + 1) * n_d * pairs]
 
-    pl.semaphore_wait(barrier, n_all - 1)
+    pl.semaphore_wait(barrier, n_d + n_r - 2)
 
     a_copies = []
     for k in range(1, n_r):
@@ -130,8 +128,6 @@
                 device_id=(d, to), device_id_type=MESH,
             )
         )
-    for copy in a_copies:
-        copy.start()
 
     def over_dimer(k, source, held, send, recv):
         peer, slot = partner(k, d, n_d)
@@ -159,6 +155,8 @@
         )
 
     each(n_d, lambda k: p_copy(k).start())
+    for copy in a_copies:
+        copy.start()
     for copy in a_copies:
         copy.wait_recv()
     for c in range(3):

time: 17.9 us -> 17.9 us (level)
  no operation moved by 1% of the time
where the time goes in v4:
time: 17.9 us; the launch traced here: 17.7 us
  Pallas kernels  16 us (89%)
  local copies, waits for them, and re-layouts  1.12 us (6%)
  between operations  0.64 us (4%)
    pallas_call x1, Pallas kernels, on_device(): pl.pallas_call(functools.partial(kernel, n_d, n_r), out_shape=(jax.ShapeD...  16 us
    unnamed x1, local copies, waits for them, and re-layouts  0.6 us
    slice x1, local copies, waits for them, and re-layouts, on_device(): return (forces, scalars[1, 0], scalars[0, 0])  0.52 us

profile of v4, /device:TPU:0, one launch (start us, length us, event | category | flops | bytes accessed | tf_op | source)
XLA Modules:
  0.0 17.7 jit_solution(7233022957269130867)
XLA Ops:
  0.6 16.0 %shard_map.85 = (f32[3,512]{1,0:T(4,128)S(1)}, f32[2,128]{1,0:T(2,128)S(1)}) custom-call(bf16[32,3,64,128]{3,2,1,0:T(8,128)(2,1)} %bitcast.5, bf16[32,64]{1,0:T(8,128)(2,1)} %refs_0_.1, bf16[32,64]{1,0:T(8,128)(2,1)} %refs_1_.1, f32[3,512]{1,0:T(4,128)} %refs_2_.1, s32[2,32]{1,0:T(2,128)} %bitcast.6, s32[2,32]{1,0:T(2,128)} %bitcast.7), custom_call_target="tpu_custom_call" | custom-call | tf_op jit(solution)/shard_map/pallas_call | solution.py:213
  16.6 0.5 %fusion = (f32[1,1]{1,0:T(1,128)}, f32[1,1]{1,0:T(1,128)}) fusion(f32[2,128]{1,0:T(2,128)S(1)} %get-tuple-element.6), kind=kLoop, calls=%fused_computation | loop fusion | bytes 16 | tf_op jit(solution)/shard_map/slice | solution.py:246
  17.1 0.6 %copy.10 = f32[3,512]{1,0:T(4,128)} copy(f32[3,512]{1,0:T(4,128)S(1)} %get-tuple-element.12) | data formatting | bytes 12288

commit v5 on v4

--- a/solution.py
+++ b/solution.py
@@ -133,12 +133,12 @@
         peer, slot = partner(k, d, n_d)
         return pltpu.make_async_remote_copy(
             src_ref=source(peer), dst_ref=held.at[slot],
-            send_sem=send.at[k], recv_sem=recv.at[slot],
+            send_sem=send, recv_sem=recv,
             device_id=(peer, r), device_id_type=MESH,
         )
 
-    def arrived(k, held, recv):
-        pltpu.make_async_copy(held.at[k], held.at[k], recv.at[k]).wait()
+    def all_of(held, semaphore):
+        pltpu.make_async_copy(held, held, semaphore).wait()
 
     def p_copy(k):
         return over_dimer(k, lambda peer: posb, in_p, p_send, p_recv)
@@ -150,7 +150,7 @@
         peer, slot = partner(k, me, n_all)
         return pltpu.make_async_remote_copy(
             src_ref=sbuf, dst_ref=in_s.at[slot],
-            send_sem=s_send.at[k], recv_sem=s_recv.at[slot],
+            send_sem=s_send, recv_sem=s_recv,
             device_id=(peer // n_r, lax.rem(peer, n_r)), device_id_type=MESH,
         )
 
@@ -166,7 +166,7 @@
         for o in range(n_d):
             acc[o, c * pairs : (c + 1) * pairs] = total[o * pairs : (o + 1) * pairs]
     each(n_d, lambda k: b_copy(k).start())
-    each(n_d, lambda k: arrived(k, in_p, p_recv))
+    all_of(in_p, p_recv)
 
     def virial_of(k, carry):
         return carry + acc[k + (k + n_d - d) // n_d] * in_p[k]
@@ -182,16 +182,16 @@
 
     for copy in a_copies:
         copy.wait_send()
-    each(n_d, lambda k: p_copy(k).wait_send())
-    each(n_d, lambda k: arrived(k, in_b, b_recv))
+    all_of(in_p, p_send)
+    all_of(in_b, b_recv)
     total = acc[d] + jnp.sum(in_b[...], axis=0)
     for c in range(3):
         for j in range(pairs):
             forces[c : c + 1, j * lanes : (j + 1) * lanes] = total[c * pairs + j : c * pairs + j + 1]
-    each(n_d, lambda k: b_copy(k).wait_send())
-    each(n_all, lambda k: s_copy(k).wait_send())
-
-    each(n_all, lambda k: arrived(k, in_s, s_recv))
+    all_of(in_b, b_send)
+    all_of(in_s, s_send)
+
+    all_of(in_s, s_recv)
     both = sbuf[...] + jnp.sum(in_s[...], axis=0)
     both = jnp.sum(both, axis=1, keepdims=True)
     row = lax.broadcasted_iota(jnp.int32, both.shape, 0)
@@ -235,9 +235,7 @@
             pltpu.VMEM((n_all - 1, 2, lanes), F32),
             dma((8,)),
             dma((n_r - 1,)), dma((n_r - 1,)),
-            dma((n_d - 1,)), dma((n_d - 1,)),
-            dma((n_d - 1,)), dma((n_d - 1,)),
-            dma((n_all - 1,)), dma((n_all - 1,)),
+            dma, dma, dma, dma, dma, dma,
         ],
         compiler_params=pltpu.CompilerParams(
             collective_id=0, has_side_effects=True, vmem_limit_bytes=room

time: 17.9 us -> 17.1 us (0.955)
  Pallas kernels: 16 us -> 15.2 us
    pallas_call x1, Pallas kernels: 16 us -> 15.2 us  [on_device(): pl.pallas_call(functools.partial(kernel, n_d, n_r), out_shape=(jax.ShapeD...]
where the time goes in v5:
time: 17.1 us; the launch traced here: 17 us
  Pallas kernels  15.2 us (89%)
  local copies, waits for them, and re-layouts  1.12 us (7%)
  between operations  0.64 us (4%)
    pallas_call x1, Pallas kernels, on_device(): pl.pallas_call(functools.partial(kernel, n_d, n_r), out_shape=(jax.ShapeD...  15.2 us
    unnamed x1, local copies, waits for them, and re-layouts  0.6 us
    slice x1, local copies, waits for them, and re-layouts, on_device(): return (forces, scalars[1, 0], scalars[0, 0])  0.52 us

profile of v5, /device:TPU:0, one launch (start us, length us, event | category | flops | bytes accessed | tf_op | source)
XLA Modules:
  0.0 17.0 jit_solution(11919027380782397538)
XLA Ops:
  0.6 15.2 %shard_map.85 = (f32[3,512]{1,0:T(4,128)S(1)}, f32[2,128]{1,0:T(2,128)S(1)}) custom-call(bf16[32,3,64,128]{3,2,1,0:T(8,128)(2,1)} %bitcast.5, bf16[32,64]{1,0:T(8,128)(2,1)} %refs_0_.1, bf16[32,64]{1,0:T(8,128)(2,1)} %refs_1_.1, f32[3,512]{1,0:T(4,128)} %refs_2_.1, s32[2,32]{1,0:T(2,128)} %bitcast.6, s32[2,32]{1,0:T(2,128)} %bitcast.7), custom_call_target="tpu_custom_call" | custom-call | tf_op jit(solution)/shard_map/pallas_call | solution.py:213
  15.9 0.5 %fusion = (f32[1,1]{1,0:T(1,128)}, f32[1,1]{1,0:T(1,128)}) fusion(f32[2,128]{1,0:T(2,128)S(1)} %get-tuple-element.6), kind=kLoop, calls=%fused_computation | loop fusion | bytes 16 | tf_op jit(solution)/shard_map/slice | solution.py:244
  16.4 0.6 %copy.10 = f32[3,512]{1,0:T(4,128)} copy(f32[3,512]{1,0:T(4,128)S(1)} %get-tuple-element.12) | data formatting | bytes 12288

commit v6 on v5

--- a/solution.py
+++ b/solution.py
@@ -30,10 +30,14 @@
     me = d * n_r + r
 
     def partner(step, mine, count):
-        flip = (2 * mine) // count
+        flip = lax.div(2 * mine, count)
         at = flip * step + (1 - flip) * (count - 2 - step)
-        peer = at + (at + count - mine) // count
-        return peer, mine - (mine + count - 1 - peer) // count
+        peer = at + lax.div(at + count - mine, count)
+        return peer, mine - lax.div(mine + count - 1 - peer, count)
+
+    def over(peer):
+        row = lax.div(peer, n_r)
+        return row, peer - row * n_r
 
     def each(count, act):
         if count <= 64:
@@ -124,7 +128,7 @@
         a_copies.append(
             pltpu.make_async_remote_copy(
                 src_ref=dbuf.at[to], dst_ref=in_a.at[k - 1],
-                send_sem=a_send.at[k - 1], recv_sem=a_recv.at[k - 1],
+                send_sem=a_send, recv_sem=a_recv,
                 device_id=(d, to), device_id_type=MESH,
             )
         )
@@ -151,14 +155,13 @@
         return pltpu.make_async_remote_copy(
             src_ref=sbuf, dst_ref=in_s.at[slot],
             send_sem=s_send, recv_sem=s_recv,
-            device_id=(peer // n_r, lax.rem(peer, n_r)), device_id_type=MESH,
+            device_id=over(peer), device_id_type=MESH,
         )
 
     each(n_d, lambda k: p_copy(k).start())
     for copy in a_copies:
         copy.start()
-    for copy in a_copies:
-        copy.wait_recv()
+    all_of(in_a, a_recv)
     for c in range(3):
         total = dbuf[r, c]
         for k in range(n_r - 1):
@@ -169,7 +172,7 @@
     all_of(in_p, p_recv)
 
     def virial_of(k, carry):
-        return carry + acc[k + (k + n_d - d) // n_d] * in_p[k]
+        return carry + acc[k + lax.div(k + n_d - d, n_d)] * in_p[k]
 
     products = acc[d] * posb[...]
     if n_d <= 64:
@@ -180,8 +183,7 @@
     sbuf[0:1] = jnp.sum(products, axis=0, keepdims=True)
     each(n_all, lambda k: s_copy(k).start())
 
-    for copy in a_copies:
-        copy.wait_send()
+    all_of(in_a, a_send)
     all_of(in_p, p_send)
     all_of(in_b, b_recv)
     total = acc[d] + jnp.sum(in_b[...], axis=0)
@@ -234,8 +236,7 @@
             pltpu.VMEM((2, lanes), F32),
             pltpu.VMEM((n_all - 1, 2, lanes), F32),
             dma((8,)),
-            dma((n_r - 1,)), dma((n_r - 1,)),
-            dma, dma, dma, dma, dma, dma,
+            dma, dma, dma, dma, dma, dma, dma, dma,
         ],
         compiler_params=pltpu.CompilerParams(
             collective_id=0, has_side_effects=True, vmem_limit_bytes=room

time: 17.1 us -> 17.1 us (level)
  no operation moved by 1% of the time
where the time goes in v6:
time: 17.1 us; the launch traced here: 16.9 us
  Pallas kernels  15.2 us (89%)
  local copies, waits for them, and re-layouts  1.12 us (7%)
  between operations  0.64 us (4%)
    pallas_call x1, Pallas kernels, on_device(): pl.pallas_call(functools.partial(kernel, n_d, n_r), out_shape=(jax.ShapeD...  15.2 us
    unnamed x1, local copies, waits for them, and re-layouts  0.6 us
    slice x1, local copies, waits for them, and re-layouts, on_device(): return (forces, scalars[1, 0], scalars[0, 0])  0.52 us

profile of v6, /device:TPU:0, one launch (start us, length us, event | category | flops | bytes accessed | tf_op | source)
XLA Modules:
  0.0 16.9 jit_solution(16411407381405084003)
XLA Ops:
  0.6 15.2 %shard_map.85 = (f32[3,512]{1,0:T(4,128)S(1)}, f32[2,128]{1,0:T(2,128)S(1)}) custom-call(bf16[32,3,64,128]{3,2,1,0:T(8,128)(2,1)} %bitcast.5, bf16[32,64]{1,0:T(8,128)(2,1)} %refs_0_.1, bf16[32,64]{1,0:T(8,128)(2,1)} %refs_1_.1, f32[3,512]{1,0:T(4,128)} %refs_2_.1, s32[2,32]{1,0:T(2,128)} %bitcast.6, s32[2,32]{1,0:T(2,128)} %bitcast.7), custom_call_target="tpu_custom_call" | custom-call | tf_op jit(solution)/shard_map/pallas_call | solution.py:215
  15.8 0.5 %fusion = (f32[1,1]{1,0:T(1,128)}, f32[1,1]{1,0:T(1,128)}) fusion(f32[2,128]{1,0:T(2,128)S(1)} %get-tuple-element.6), kind=kLoop, calls=%fused_computation | loop fusion | bytes 16 | tf_op jit(solution)/shard_map/slice | solution.py:245
  16.3 0.6 %copy.10 = f32[3,512]{1,0:T(4,128)} copy(f32[3,512]{1,0:T(4,128)S(1)} %get-tuple-element.12) | data formatting | bytes 12288
